TPU v7x, 128 devices: a whole 4x4x4 slice. The times are simulated.
128 devices in a mesh: row: 8 (over x_hi, y), col: 16 (over z, x_lo, core).
Axes of the slice: x: 4 (x_hi: 2, x_lo: 2; x = x_hi * 2 + x_lo), y: 4, z: 4, core: 2. Of those that a mesh axis runs over, the one named last changes fastest.
Arguments:
- left_matrix: bfloat16 [6144, 32768], P('row', 'col'), may hold values from -6 to 6
- right_matrix: bfloat16 [32768, 8192], P('row', 'col'), may hold values from -0.078125 to 0.078125
- left_mask: int32 [48, 256], P('row', 'col'), may hold values from 0 to 1
- right_mask: int32 [256, 64], P('row', 'col'), may hold values from 0 to 1
- keep_mask: int32 [48, 64], P('row', 'col'), may hold values 0 or 1
Outputs:
- product: bfloat16 [6144, 8192], P('row', 'col')
All inputs are finite; a program needn't handle non-finite values. No bound on the sum of `keep_mask` on one device may be relied on, other than what follows from the above.
Results may differ from a plain program's by a relative error of at most 0.001.
Values may be sent and summed in bfloat16 or wider, within the bound.
No kernel may reach another device: no remote copies, remote signals or barrier semaphores. Data moves between devices by JAX's collectives and lax.ppermute only.
A program may use at most 128 MiB of HBM per device.

v0:
```python
import jax
import jax.numpy as jnp
from jax import lax
from jax.sharding import PartitionSpec as P

BLOCK = 128
TICKS = 3


def passed_along(value, axis, by):
    length = lax.axis_size(axis)
    return lax.ppermute(value, axis, [(i, (i + by) % length) for i in range(length)])


def partner(block, axis, stride):
    count = lax.axis_size(axis)
    route = []
    for low in range(count):
        high = low | 1 << stride
        if high != low and high < count:
            route += [(low, high), (high, low)]
    return lax.ppermute(block, axis, route)


def sparsify(matrix, mask):
    rows, cols = matrix.shape
    shaped = matrix.reshape(rows // BLOCK, BLOCK, cols // BLOCK, BLOCK)
    return (shaped * mask[:, None, :, None].astype(matrix.dtype)).reshape(rows, cols)


def shards(left_matrix, right_matrix, left_mask, right_mask, keep_mask):
    row_index = lax.axis_index("row")
    col_index = lax.axis_index("col")
    group = col_index // 2
    parity = col_index % 2
    levels = lax.axis_size("row").bit_length() - 1
    left_sparse = sparsify(left_matrix, left_mask)
    right_sparse = sparsify(right_matrix, right_mask)

    def join(own, other):
        lower = jnp.where(parity == 0, own, other)
        upper = jnp.where(parity == 0, other, own)
        return jnp.concatenate([lower, upper], axis=1)

    for level in range(levels):
        moved = passed_along(right_sparse, "row", -(1 << level))
        right_sparse = jnp.where((group >> level) % 2 == 1, moved, right_sparse)
    holding = left_sparse
    for level in range(levels):
        moved = passed_along(holding, "col", -(2 << level))
        holding = jnp.where((row_index >> level) % 2 == 1, moved, holding)

    def whole(state):
        return join(state, partner(state, "col", 0))

    total = jnp.dot(whole(holding), right_sparse, preferred_element_type=jnp.float32)
    for tick in range(1, TICKS):
        holding = passed_along(holding, "col", -2)
        right_sparse = passed_along(right_sparse, "row", -1)
        total = total + jnp.dot(whole(holding), right_sparse, preferred_element_type=jnp.float32)
    rows, cols = total.shape
    kept = total.reshape(rows // BLOCK, BLOCK, cols // BLOCK, BLOCK) * keep_mask[
        :, None, :, None
    ].astype(jnp.float32)
    return kept.reshape(rows, cols).astype(jnp.bfloat16)


def solution(mesh):
    placed = (P("row", "col"), P("row", "col"), P("row", "col"), P("row", "col"), P("row", "col"))
    return jax.shard_map(
        shards, mesh=mesh, in_specs=placed, out_specs=P("row", "col"), check_vma=False
    )
```

profile of v0, /device:TPU:88, one launch (start us, length us, event | category | flops | bytes accessed | tf_op | source)
XLA Modules:
  0.0 677.4 jit_solution(6898382615369633818)
XLA Ops:
  0.0 0.7 convert_element_type.16
  0.7 0.1 copy.6
  0.8 0.0 copy-start.1
  0.8 1.1 mul.36
  1.9 1.0 copy-done.1
  3.0 0.0 copy-start.5
  3.0 2.5 bitcast_multiply_fusion
  5.5 0.0 copy-start.4
  5.5 0.7 collective-permute-start.4
  6.3 0.0 copy-done.5
  6.3 0.5 mul.33
  6.8 0.7 copy-done.4
  7.4 0.7 bitcast_multiply_fusion.1
  8.1 1.1 collective-permute-start
  9.2 93.7 %collective-permute-done.4 = bf16[4096,512]{1,0:T(8,128)(2,1)} collective-permute-done((bf16[4096,512]{1,0:T(8,128)(2,1)}, bf16[4096,512]{1,0:T(8,128)(2,1)}, u32[]{:S(2)}, u32[]{:S(2)}) %collective-permute-start.4) | collective-permute-done | bytes 4194336 | tf_op jit(solution)/shard_map/ppermute | solution.py:12
  102.9 4.6 broadcast_select_fusion
  107.5 0.0 collective-permute-start.5
  107.5 0.0 collective-permute-done
  107.5 4.0 broadcast_select_fusion.3
  111.5 0.1 collective-permute-start.1
  111.6 68.1 %collective-permute-done.1 = bf16[768,2048]{1,0:T(8,128)(2,1)} collective-permute-done((bf16[768,2048]{1,0:T(8,128)(2,1)}, bf16[768,2048]{1,0:T(8,128)(2,1)}, u32[]{:S(2)}, u32[]{:S(2)}) %collective-permute-start.1) | collective-permute-done | bytes 3145760 | tf_op jit(solution)/shard_map/ppermute | solution.py:12
  179.7 2.2 broadcast_select_fusion.4
  181.9 0.0 copy-start
  181.9 1.3 collective-permute-start.2
  183.2 18.9 %collective-permute-done.5 = bf16[4096,512]{1,0:T(8,128)(2,1)} collective-permute-done((bf16[4096,512]{1,0:T(8,128)(2,1)}, bf16[4096,512]{1,0:T(8,128)(2,1)}, u32[]{:S(2)}, u32[]{:S(2)}) %collective-permute-start.5) | collective-permute-done | bytes 4194336 | tf_op jit(solution)/shard_map/ppermute | solution.py:12
  202.1 4.6 broadcast_select_fusion.1
  206.7 0.0 copy-done
  206.7 3.0 collective-permute-start.6
  209.7 40.9 %collective-permute-done.2 = bf16[768,2048]{1,0:T(8,128)(2,1)} collective-permute-done((bf16[768,2048]{1,0:T(8,128)(2,1)S(1)}, bf16[768,2048]{1,0:T(8,128)(2,1)}, u32[]{:S(2)}, u32[]{:S(2)}) %collective-permute-start.2) | collective-permute-done | bytes 3145760 | tf_op jit(solution)/shard_map/ppermute | solution.py:12
  250.6 2.2 broadcast_select_fusion.5
  252.8 2.0 collective-permute-start.7
  254.9 0.0 copy-start.6
  254.9 47.1 %collective-permute-done.6 = bf16[4096,512]{1,0:T(8,128)(2,1)} collective-permute-done((bf16[4096,512]{1,0:T(8,128)(2,1)}, bf16[4096,512]{1,0:T(8,128)(2,1)}, u32[]{:S(2)}, u32[]{:S(2)}) %collective-permute-start.6) | collective-permute-done | bytes 4194336 | tf_op jit(solution)/shard_map/ppermute | solution.py:12
  302.0 2.6 broadcast_select_fusion.2
  304.6 0.0 copy-start.2
  304.6 57.9 %collective-permute-start.9 = (bf16[4096,512]{1,0:T(8,128)(2,1)S(1)}, bf16[4096,512]{1,0:T(8,128)(2,1)}, u32[]{:S(2)}, u32[]{:S(2)}) collective-permute-start(bf16[4096,512]{1,0:T(8,128)(2,1)S(1)} %broadcast_select_fusion.2), channel_id=1, source_target_pairs={{0,112},{16,0},{32,16},{48,32},{64,48},{80,64},{96,80},{112,96},{1... | collective-permute-start | bytes 12582920 | tf_op jit(solution)/shard_map/ppermute | solution.py:12
  362.5 3.2 collective-permute-done.7
  365.7 0.0 copy-done.2
  365.7 2.2 collective-permute-start.10
  367.9 0.0 collective-permute-start.3
  367.9 0.5 collective-permute-start.8
  368.4 146.9 %collective-permute-done.9 = bf16[4096,512]{1,0:T(8,128)(2,1)} collective-permute-done((bf16[4096,512]{1,0:T(8,128)(2,1)S(1)}, bf16[4096,512]{1,0:T(8,128)(2,1)}, u32[]{:S(2)}, u32[]{:S(2)}) %collective-permute-start.9) | collective-permute-done | bytes 4194336 | tf_op jit(solution)/shard_map/ppermute | solution.py:12
  515.3 0.0 collective-permute-start.12
  515.3 0.0 copy-done.6
  515.3 0.1 copy.7
  515.4 0.0 copy-start.3
  515.4 0.0 collective-permute-done.10
  515.4 0.2 collective-permute-start.11
  515.6 0.0 collective-permute-done.3
  515.7 2.5 broadcast_select_fusion.11
  518.1 0.4 copy-done.3
  518.5 3.4 fusion
  521.9 0.0 collective-permute-done.8
  521.9 3.3 broadcast_select_fusion.9
  525.2 5.6 fusion.4
  530.8 0.0 collective-permute-done.11
  530.8 2.3 broadcast_select_fusion.7
  533.1 137.5 %collective-permute-done.12 = bf16[4096,512]{1,0:T(8,128)(2,1)} collective-permute-done((bf16[4096,512]{1,0:T(8,128)(2,1)}, bf16[4096,512]{1,0:T(8,128)(2,1)}, u32[]{:S(2)}, u32[]{:S(2)}) %collective-permute-start.12) | collective-permute-done | bytes 4194336 | tf_op jit(solution)/shard_map/ppermute | solution.py:12
  670.6 0.3 mul.39
  670.9 6.5 fusion.12
  (2 shorter events, 0.0 us)
Async XLA Ops:
  0.8 2.2 copy-start.1
  3.0 3.3 copy-start.5
  5.5 1.9 copy-start.4
  5.5 97.4 %collective-permute-start.4 = (bf16[4096,512]{1,0:T(8,128)(2,1)}, bf16[4096,512]{1,0:T(8,128)(2,1)}, u32[]{:S(2)}, u32[]{:S(2)}) collective-permute-start(bf16[4096,512]{1,0:T(8,128)(2,1)} %bitcast_multiply_fusion), channel_id=1, source_target_pairs={{0,112},{16,0},{32,16},{48,32},{64,48},{80,64},{96,80},{112,96},{1... | collective-permute-start | bytes 12582920 | tf_op jit(solution)/shard_map/ppermute | solution.py:12
  8.1 99.4 %collective-permute-start = (bf16[768,2048]{1,0:T(8,128)(2,1)S(1)}, bf16[768,2048]{1,0:T(8,128)(2,1)}, u32[]{:S(2)}, u32[]{:S(2)}) collective-permute-start(bf16[768,2048]{1,0:T(8,128)(2,1)S(1)} %bitcast_multiply_fusion.1), channel_id=1, source_target_pairs={{0,14},{1,15},{2,0},{3,1},{4,2},{5,3},{6,4},{7,5},{8,6},{9,7},{10,... | collective-permute-start | bytes 9437192 | tf_op jit(solution)/shard_map/ppermute | solution.py:12
  107.5 94.5 %collective-permute-start.5 = (bf16[4096,512]{1,0:T(8,128)(2,1)}, bf16[4096,512]{1,0:T(8,128)(2,1)}, u32[]{:S(2)}, u32[]{:S(2)}) collective-permute-start(bf16[4096,512]{1,0:T(8,128)(2,1)} %broadcast_select_fusion), channel_id=1, source_target_pairs={{0,96},{16,112},{32,0},{48,16},{64,32},{80,48},{96,64},{112,80},{1... | collective-permute-start | bytes 12582920 | tf_op jit(solution)/shard_map/ppermute | solution.py:12
  111.5 68.2 %collective-permute-start.1 = (bf16[768,2048]{1,0:T(8,128)(2,1)}, bf16[768,2048]{1,0:T(8,128)(2,1)}, u32[]{:S(2)}, u32[]{:S(2)}) collective-permute-start(bf16[768,2048]{1,0:T(8,128)(2,1)} %broadcast_select_fusion.3), channel_id=1, source_target_pairs={{0,12},{1,13},{2,14},{3,15},{4,0},{5,1},{6,2},{7,3},{8,4},{9,5},{1... | collective-permute-start | bytes 9437192 | tf_op jit(solution)/shard_map/ppermute | solution.py:12
  181.9 24.8 %copy-start = (bf16[768,2048]{1,0:T(8,128)(2,1)}, bf16[768,2048]{1,0:T(8,128)(2,1)S(1)}, u32[]{:S(2)}) copy-start(bf16[768,2048]{1,0:T(8,128)(2,1)S(1)} %broadcast_select_fusion.4) | copy-start | bytes 9437188
  181.9 68.7 %collective-permute-start.2 = (bf16[768,2048]{1,0:T(8,128)(2,1)S(1)}, bf16[768,2048]{1,0:T(8,128)(2,1)}, u32[]{:S(2)}, u32[]{:S(2)}) collective-permute-start(bf16[768,2048]{1,0:T(8,128)(2,1)S(1)} %broadcast_select_fusion.4), channel_id=1, source_target_pairs={{0,8},{1,9},{2,10},{3,11},{4,12},{5,13},{6,14},{7,15},{8,0},{9,1},... | collective-permute-start | bytes 9437192 | tf_op jit(solution)/shard_map/ppermute | solution.py:12
  206.7 95.3 %collective-permute-start.6 = (bf16[4096,512]{1,0:T(8,128)(2,1)}, bf16[4096,512]{1,0:T(8,128)(2,1)}, u32[]{:S(2)}, u32[]{:S(2)}) collective-permute-start(bf16[4096,512]{1,0:T(8,128)(2,1)} %broadcast_select_fusion.1), channel_id=1, source_target_pairs={{0,64},{16,80},{32,96},{48,112},{64,0},{80,16},{96,32},{112,48},{1... | collective-permute-start | bytes 12582920 | tf_op jit(solution)/shard_map/ppermute | solution.py:12
  252.8 112.9 %collective-permute-start.7 = (bf16[768,2048]{1,0:T(8,128)(2,1)S(1)}, bf16[768,2048]{1,0:T(8,128)(2,1)}, u32[]{:S(2)}, u32[]{:S(2)}) collective-permute-start(bf16[768,2048]{1,0:T(8,128)(2,1)S(1)} %broadcast_select_fusion.5), channel_id=1, source_target_pairs={{0,14},{1,15},{2,0},{3,1},{4,2},{5,3},{6,4},{7,5},{8,6},{9,7},{10,... | collective-permute-start | bytes 9437192 | tf_op jit(solution)/shard_map/ppermute | solution.py:12
  254.9 260.4 %copy-start.6 = (s32[6,4]{0,1:T(4,128)S(1)}, s32[6,4]{0,1:T(4,128)}, u32[]{:S(2)}) copy-start(s32[6,4]{0,1:T(4,128)} %param.9) | copy-start | bytes 292
  304.6 61.1 %copy-start.2 = (bf16[4096,512]{1,0:T(8,128)(2,1)}, bf16[4096,512]{1,0:T(8,128)(2,1)S(1)}, u32[]{:S(2)}) copy-start(bf16[4096,512]{1,0:T(8,128)(2,1)S(1)} %broadcast_select_fusion.2) | copy-start | bytes 12582916
  304.6 210.7 %collective-permute-start.9 = (bf16[4096,512]{1,0:T(8,128)(2,1)S(1)}, bf16[4096,512]{1,0:T(8,128)(2,1)}, u32[]{:S(2)}, u32[]{:S(2)}) collective-permute-start(bf16[4096,512]{1,0:T(8,128)(2,1)S(1)} %broadcast_select_fusion.2), channel_id=1, source_target_pairs={{0,112},{16,0},{32,16},{48,32},{64,48},{80,64},{96,80},{112,96},{1... | collective-permute-start | bytes 12582920 | tf_op jit(solution)/shard_map/ppermute | solution.py:12
  365.7 149.7 %collective-permute-start.10 = (bf16[768,2048]{1,0:T(8,128)(2,1)}, bf16[768,2048]{1,0:T(8,128)(2,1)}, u32[]{:S(2)}, u32[]{:S(2)}) collective-permute-start(bf16[768,2048]{1,0:T(8,128)(2,1)} %collective-permute-done.7), channel_id=1, source_target_pairs={{0,14},{1,15},{2,0},{3,1},{4,2},{5,3},{6,4},{7,5},{8,6},{9,7},{10,... | collective-permute-start | bytes 9437192 | tf_op jit(solution)/shard_map/ppermute | solution.py:12
  367.9 147.8 %collective-permute-start.3 = (bf16[768,2048]{1,0:T(8,128)(2,1)S(1)}, bf16[768,2048]{1,0:T(8,128)(2,1)}, u32[]{:S(2)}, u32[]{:S(2)}) collective-permute-start(bf16[768,2048]{1,0:T(8,128)(2,1)S(1)} %broadcast_select_fusion.5), channel_id=1, source_target_pairs={{0,1},{1,0},{2,3},{3,2},{4,5},{5,4},{6,7},{7,6},{8,9},{9,8},{10,11... | collective-permute-start | bytes 9437192 | tf_op jit(solution)/shard_map/ppermute | solution.py:22
  367.9 154.1 %collective-permute-start.8 = (bf16[768,2048]{1,0:T(8,128)(2,1)}, bf16[768,2048]{1,0:T(8,128)(2,1)}, u32[]{:S(2)}, u32[]{:S(2)}) collective-permute-start(bf16[768,2048]{1,0:T(8,128)(2,1)} %collective-permute-done.7), channel_id=1, source_target_pairs={{0,1},{1,0},{2,3},{3,2},{4,5},{5,4},{6,7},{7,6},{8,9},{9,8},{10,11... | collective-permute-start | bytes 9437192 | tf_op jit(solution)/shard_map/ppermute | solution.py:22
  515.3 155.3 %collective-permute-start.12 = (bf16[4096,512]{1,0:T(8,128)(2,1)}, bf16[4096,512]{1,0:T(8,128)(2,1)}, u32[]{:S(2)}, u32[]{:S(2)}) collective-permute-start(bf16[4096,512]{1,0:T(8,128)(2,1)} %collective-permute-done.9), channel_id=1, source_target_pairs={{0,112},{16,0},{32,16},{48,32},{64,48},{80,64},{96,80},{112,96},{1... | collective-permute-start | bytes 12582920 | tf_op jit(solution)/shard_map/ppermute | solution.py:12
  515.4 3.1 copy-start.3
  515.4 15.4 %collective-permute-start.11 = (bf16[768,2048]{1,0:T(8,128)(2,1)}, bf16[768,2048]{1,0:T(8,128)(2,1)S(1)}, u32[]{:S(2)}, u32[]{:S(2)}) collective-permute-start(bf16[768,2048]{1,0:T(8,128)(2,1)} %collective-permute-done.10), channel_id=1, source_target_pairs={{0,1},{1,0},{2,3},{3,2},{4,5},{5,4},{6,7},{7,6},{8,9},{9,8},{10,11... | collective-permute-start | bytes 9437192 | tf_op jit(solution)/shard_map/ppermute | solution.py:22
where the time goes:
time: 678 us; the launch traced here: 677 us
  waiting for transfers between devices  556 us (82%)
  starting transfers between devices  69.2 us (10%)
  other arithmetic  32.2 us (5%)
  matrix products  15.5 us (2%)
    ppermute x10, waiting for transfers between devices, passed_along(): lax.ppermute(value, axis, [(i, (i + by) % length) for i in range(length)])  556 us
    ppermute x10, starting transfers between devices, passed_along(): lax.ppermute(value, axis, [(i, (i + by) % length) for i in range(length)])  68.4 us
    dot_general x3, matrix products, shards(): jnp.dot(whole(holding), right_sparse, preferred_element_type=jnp.float32)  15.5 us
  transfers between devices with their start and end apart: 13, of which 8 were waited for; matrix products, arithmetic and copies ran while one was open for 6% of the time, Pallas kernels for 0%

commit v1 on v0

v1 whole, which is shorter than its diff:
```python
import jax
import jax.numpy as jnp
from jax import lax
from jax.experimental import pallas as pl
from jax.experimental.pallas import tpu as pltpu
from jax.sharding import PartitionSpec as P

BLOCK = 128
TICKS = 3
ROWS = 8
HALF = 4
COLS = 16
UNITS = 8
ROW_CUTS = 2
COL_CUTS = 2


def send(value, route, where=lambda row, col: True):
    pairs = []
    for row in range(ROWS):
        for col in range(COLS):
            if where(row, col):
                to_row, to_col = route(row, col)
                pairs.append((row * COLS + col, to_row * COLS + to_col))
    return lax.ppermute(value, ("row", "col"), pairs)


def at(group, core):
    return 2 * (group % UNITS) + core


def skewed(row, col):
    unit, core = divmod(col, 2)
    first = (unit - row) % UNITS
    if row % 2:
        group = first - 1
    else:
        group = first if first % 2 else first - 2
    return HALF * (unit // HALF) + row % HALF, at(group, core)


def swapped(row, col):
    group, core = divmod(col, 2)
    return row, at(group ^ 1, core)


def lifted(row, col):
    group, core = divmod(col, 2)
    return row, at(group - 2 if group % 2 else group + 2, core)


def partner(row, col):
    return row, col ^ 1


def mirrored(row, col):
    return (row + HALF) % ROWS, col


def along(by):
    return lambda row, col: (row // HALF * HALF + (row + by) % HALF, col)


def sparsify(matrix, mask):
    rows, cols = matrix.shape
    shaped = matrix.reshape(rows // BLOCK, BLOCK, cols // BLOCK, BLOCK)
    return (shaped * mask[:, None, :, None].astype(matrix.dtype)).reshape(rows, cols)


def products(table, lefts, rights):
    rows, depth = lefts[0].shape
    cols = rights[0].shape[1]
    steps = [(piece, half) for piece in range(TICKS) for half in range(2)]

    def kernel(table_ref, *refs):
        left_refs, right_refs = refs[:8], refs[8:13]
        own_ref, mirror_ref, left_buf, right_buf, acc_ref, left_sem, right_sem = refs[13:]
        core, odd = table_ref[0], table_ref[1]

        def left_copy(source, step):
            return pltpu.make_async_copy(source, left_buf.at[step], left_sem.at[step])

        def right_copy(source, step):
            return pltpu.make_async_copy(source, right_buf.at[step], right_sem.at[step])

        for step, (piece, half) in enumerate(steps):
            for other in range(2):
                mine = core == half if other == 0 else core != half
                if piece < 2:
                    @pl.when(mine)
                    def _():
                        left_copy(left_refs[2 * piece + other], step).start()
                else:
                    for parity in range(2):
                        @pl.when(jnp.logical_and(mine, odd == parity))
                        def _():
                            left_copy(left_refs[4 + 2 * parity + other], step).start()
            offset = table_ref[2 + piece]
            for which, ref in ((0, right_refs[0]), (1, right_refs[1]), (3, right_refs[2])):
                @pl.when(offset == which)
                def _():
                    right_copy(ref.at[pl.ds(half * depth, depth), :], step).start()

            @pl.when(offset == 2)
            def _():
                right_copy(right_refs[3 + half], step).start()
        acc_ref[...] = jnp.zeros_like(acc_ref)
        for step, (piece, half) in enumerate(steps):
            left_copy(left_refs[0], step).wait()
            right_copy(right_refs[3], step).wait()
            part = jnp.dot(left_buf[step], right_buf[step], preferred_element_type=jnp.float32)
            acc_ref[table_ref[5 + piece]] += part
        own_ref[...] = acc_ref[0]
        mirror_ref[...] = acc_ref[1]

    hbm = pl.BlockSpec(memory_space=pl.ANY)
    count = len(steps)
    return pl.pallas_call(
        kernel,
        out_shape=[jax.ShapeDtypeStruct((rows, cols), jnp.float32)] * 2,
        in_specs=[pl.BlockSpec(memory_space=pltpu.SMEM)] + [hbm] * 13,
        out_specs=[pl.BlockSpec(memory_space=pltpu.VMEM)] * 2,
        scratch_shapes=[
            pltpu.VMEM((count, rows, depth), jnp.bfloat16),
            pltpu.VMEM((count, depth, cols), jnp.bfloat16),
            pltpu.VMEM((2, rows, cols), jnp.float32),
            pltpu.SemaphoreType.DMA((count,)),
            pltpu.SemaphoreType.DMA((count,)),
        ],
        compiler_params=pltpu.CompilerParams(vmem_limit_bytes=48 << 20),
        cost_estimate=pl.CostEstimate(
            flops=2 * count * rows * depth * cols,
            bytes_accessed=2 * count * depth * (rows + cols),
            transcendentals=0,
        ),
    )(table, *lefts, *rights)


def shards(left_matrix, right_matrix, left_mask, right_mask, keep_mask):
    row = lax.axis_index("row")
    col = lax.axis_index("col")
    high = row % HALF
    group = col // 2
    odd = row % 2
    parity = group % 2
    ticks = [
        jnp.where(odd == 0, jnp.where(parity == 0, 2, 0), 1),
        jnp.where(odd == 0, 1, jnp.where(parity == 0, 2, 0)),
        jnp.where(parity == 0, 0, 2),
    ]
    offsets = [(group + tick) % HALF for tick in ticks]
    sides = [(high + group + tick) // HALF % 2 for tick in ticks]
    table = jnp.stack([col % 2, odd] + offsets + sides).astype(jnp.int32)

    rights = []
    cols = right_matrix.shape[1] // COL_CUTS
    for cut in range(COL_CUTS):
        blocks = cols // BLOCK
        piece = sparsify(
            right_matrix[:, cut * cols:(cut + 1) * cols],
            right_mask[:, cut * blocks:(cut + 1) * blocks],
        )
        after = send(piece, along(-1))
        before = send(piece, along(1))
        depth = piece.shape[0] // 2
        across = (send(before[:depth], along(1)), send(after[depth:], along(-1)))
        rights.append((piece, after, before) + across)

    lefts = []
    rows = left_matrix.shape[0] // ROW_CUTS
    for cut in range(ROW_CUTS):
        blocks = rows // BLOCK
        piece = sparsify(
            left_matrix[cut * rows:(cut + 1) * rows],
            left_mask[cut * blocks:(cut + 1) * blocks],
        )
        first = send(piece, skewed)
        second = send(first, swapped)
        even = send(first, lifted, lambda row, col: row % 2 == 0)
        uneven = send(second, lifted, lambda row, col: row % 2 == 1)
        lefts.append([part for own in (first, second, even, uneven) for part in (own, send(own, partner))])

    bands = []
    for cut in range(ROW_CUTS):
        band = []
        for side in range(COL_CUTS):
            own, mirror = products(table, lefts[cut], rights[side])
            band.append(own + send(mirror, mirrored))
        bands.append(jnp.concatenate(band, axis=1))
    total = jnp.concatenate(bands, axis=0)
    rows, cols = total.shape
    kept = total.reshape(rows // BLOCK, BLOCK, cols // BLOCK, BLOCK) * keep_mask[
        :, None, :, None
    ].astype(jnp.float32)
    return kept.reshape(rows, cols).astype(jnp.bfloat16)


def solution(mesh):
    placed = (P("row", "col"), P("row", "col"), P("row", "col"), P("row", "col"), P("row", "col"))
    return jax.shard_map(
        shards, mesh=mesh, in_specs=placed, out_specs=P("row", "col"), check_vma=False
    )
```

time: 678 us -> 275 us (0.41)
  waiting for transfers between devices: 556 us -> 176 us
  Pallas kernels: 0 us -> 33.5 us
  starting transfers between devices: 69.2 us -> 36 us
  other arithmetic: 32.2 us -> 8.45 us
  matrix products: 15.5 us -> 0 us
  local copies, waits for them, and re-layouts: 4.22 us -> 17 us
    ppermute x13 -> x28, waiting for transfers between devices: 556 us -> 176 us  [send(): return lax.ppermute(value, ('row', 'col'), pairs)]
    pallas_call x0 -> x4, Pallas kernels: none -> 33.5 us  [products(): pl.pallas_call(kernel, out_shape=[jax.ShapeDtypeStruct((rows, cols), jnp....]
    ppermute x13 -> x28, starting transfers between devices: 69.2 us -> 36 us  [send(): return lax.ppermute(value, ('row', 'col'), pairs)]
    select_n x9 -> x0, other arithmetic: 28.3 us -> none  [the longest x3 11.9 us: shards(): right_sparse = jnp.where((group >> level) % 2 == 1, moved, right_sparse)]
    dot_general x3 -> x0, matrix products: 15.5 us -> none  [shards(): jnp.dot(whole(holding), right_sparse, preferred_element_type=jnp.float32)]
    unnamed x14 -> x58, local copies, waits for them, and re-layouts: 2.13 us -> 12.3 us
  transfers between devices with their start and end apart: 13 -> 28, of which waited for: 8 -> 12; matrix products, arithmetic and copies ran while one was open for 6% -> 3% of each run, Pallas kernels for 0% -> 12%
where the time goes in v1:
time: 275 us; the launch traced here: 272 us
  waiting for transfers between devices  176 us (64%)
  starting transfers between devices  36 us (13%)
  Pallas kernels  33.5 us (12%)
  local copies, waits for them, and re-layouts  17 us (6%)
  other arithmetic  8.45 us (3%)
    ppermute x28, waiting for transfers between devices, send(): return lax.ppermute(value, ('row', 'col'), pairs)  176 us
    ppermute x28, starting transfers between devices, send(): return lax.ppermute(value, ('row', 'col'), pairs)  36 us
    pallas_call x4, Pallas kernels, products(): pl.pallas_call(kernel, out_shape=[jax.ShapeDtypeStruct((rows, cols), jnp....  33.5 us
    unnamed x58, local copies, waits for them, and re-layouts  12.3 us
  transfers between devices with their start and end apart: 28, of which 12 were waited for; matrix products, arithmetic and copies ran while one was open for 3% of the time, Pallas kernels for 12%

profile of v1, /device:TPU:88, one launch (start us, length us, event | category | flops | bytes accessed | tf_op | source)
XLA Modules:
  0.0 271.6 jit_solution(14473538221338399317)
XLA Ops:
  0.0 0.7 convert.8
  0.7 0.3 mul.64
  1.0 0.3 mul.55
  1.3 1.3 copy-done.25
  2.6 2.4 bitcast_multiply_fusion.4
  5.0 4.0 %collective-permute-start = (bf16[384,2048]{1,0:T(8,128)(2,1)}, bf16[384,2048]{1,0:T(8,128)(2,1)S(1)}, u32[]{:S(2)}, u32[]{:S(2)}) collective-permute-start(bf16[384,2048]{1,0:T(8,128)(2,1)} %get-tuple-element.23), channel_id=1, source_target_pairs={{0,12},{1,13},{2,2},{3,3},{4,0},{5,1},{6,6},{7,7},{8,68},{9,69},{1... | collective-permute-start | bytes 4718600 | tf_op jit(solution)/shard_map/ppermute | solution.py:25
  9.1 0.1 copy.6
  9.2 0.1 copy.7
  9.3 1.1 mul.58
  10.4 1.1 mul.61
  11.6 1.1 bitcast_multiply_fusion.1
  12.7 0.7 collective-permute-start.9
  13.4 1.3 collective-permute-start.8
  14.8 2.4 collective-permute-start.18
  17.2 3.3 %collective-permute-start.14 = (bf16[4096,256]{1,0:T(8,128)(2,1)S(1)}, bf16[4096,256]{1,0:T(8,128)(2,1)S(1)}, u32[]{:S(2)}, u32[]{:S(2)}) collective-permute-start(bf16[4096,256]{1,0:T(8,128)(2,1)S(1)} %get-tuple-element.22.refs_8_), channel_id=1, source_target_pairs={{0,16},{1,17},{2,18},{3,19},{4,20},{5,21},{6,22},{7,23},{8,24},{9,... | collective-permute-start | bytes 6291464 | tf_op jit(solution)/shard_map/ppermute | solution.py:25
  20.5 25.4 %collective-permute-done.refs_0_ = bf16[384,2048]{1,0:T(8,128)(2,1)S(1)} collective-permute-done((bf16[384,2048]{1,0:T(8,128)(2,1)}, bf16[384,2048]{1,0:T(8,128)(2,1)S(1)}, u32[]{:S(2)}, u32[]{:S(2)}) %collective-permute-start) | collective-permute-done | bytes 1572896 | tf_op jit(solution)/shard_map/ppermute | solution.py:25
  45.9 0.7 collective-permute-start.13
  46.6 14.6 %collective-permute-done.9.refs_10_ = bf16[4096,256]{1,0:T(8,128)(2,1)S(1)} collective-permute-done((bf16[4096,256]{1,0:T(8,128)(2,1)S(1)}, bf16[4096,256]{1,0:T(8,128)(2,1)S(1)}, u32[]{:S(2)}, u32[]{:S(2)}) %collective-permute-start.9) | collective-permute-done | bytes 2097184 | tf_op jit(solution)/shard_map/ppermute | solution.py:25
  61.3 0.6 collective-permute-start.2
  61.9 0.7 copy-done.14
  62.7 0.5 collective-permute-done.8.refs_9_
  63.2 1.4 collective-permute-start.10
  64.7 13.8 %collective-permute-done.18.refs_0_ = bf16[384,2048]{1,0:T(8,128)(2,1)S(1)} collective-permute-done((bf16[384,2048]{1,0:T(8,128)(2,1)S(1)}, bf16[384,2048]{1,0:T(8,128)(2,1)S(1)}, u32[]{:S(2)}, u32[]{:S(2)}) %collective-permute-start.18) | collective-permute-done | bytes 1572896 | tf_op jit(solution)/shard_map/ppermute | solution.py:25
  78.4 0.7 collective-permute-start.11
  79.2 27.0 %collective-permute-done.14.refs_10_ = bf16[4096,256]{1,0:T(8,128)(2,1)S(1)} collective-permute-done((bf16[4096,256]{1,0:T(8,128)(2,1)S(1)}, bf16[4096,256]{1,0:T(8,128)(2,1)S(1)}, u32[]{:S(2)}, u32[]{:S(2)}) %collective-permute-start.14) | collective-permute-done | bytes 2097184 | tf_op jit(solution)/shard_map/ppermute | solution.py:25
  106.2 0.8 collective-permute-start.4
  107.0 1.1 collective-permute-done.13.refs_9_
  108.1 19.2 %collective-permute-done.10.refs_11_ = bf16[2048,256]{1,0:T(8,128)(2,1)S(1)} collective-permute-done((bf16[2048,256]{1,0:T(8,128)(2,1)S(1)}, bf16[2048,256]{1,0:T(8,128)(2,1)S(1)}, u32[]{:S(2)}, u32[]{:S(2)}) %collective-permute-start.10) | collective-permute-done | bytes 1048608 | tf_op jit(solution)/shard_map/ppermute | solution.py:25
  127.3 0.6 collective-permute-start.20
  127.9 4.4 %collective-permute-start.6 = (bf16[384,2048]{1,0:T(8,128)(2,1)S(1)}, bf16[384,2048]{1,0:T(8,128)(2,1)S(1)}, u32[]{:S(2)}, u32[]{:S(2)}) collective-permute-start(bf16[384,2048]{1,0:T(8,128)(2,1)S(1)} %collective-permute-done.2.refs_2_), channel_id=1, source_target_pairs={{16,20},{17,21},{18,30},{19,31},{20,24},{21,25},{22,18},{23,19},{2... | collective-permute-start | bytes 4718600 | tf_op jit(solution)/shard_map/ppermute | solution.py:25
  132.4 1.0 copy-done.5
  133.3 23.2 %collective-permute-done.15.refs_11_ = bf16[2048,256]{1,0:T(8,128)(2,1)S(1)} collective-permute-done((bf16[2048,256]{1,0:T(8,128)(2,1)S(1)}, bf16[2048,256]{1,0:T(8,128)(2,1)S(1)}, u32[]{:S(2)}, u32[]{:S(2)}) %collective-permute-start.15) | collective-permute-done | bytes 1048608 | tf_op jit(solution)/shard_map/ppermute | solution.py:25
  156.5 0.9 copy-done.8
  157.5 1.8 collective-permute-start.22
  159.3 1.2 copy-done
  160.5 0.5 collective-permute-start.5
  161.0 1.4 collective-permute-done.20.refs_2_
  162.4 4.4 %collective-permute-start.24 = (bf16[384,2048]{1,0:T(8,128)(2,1)}, bf16[384,2048]{1,0:T(8,128)(2,1)}, u32[]{:S(2)}, u32[]{:S(2)}) collective-permute-start(bf16[384,2048]{1,0:T(8,128)(2,1)} %collective-permute-done.20.refs_2_), channel_id=1, source_target_pairs={{16,20},{17,21},{18,30},{19,31},{20,24},{21,25},{22,18},{23,19},{2... | collective-permute-start | bytes 4718600 | tf_op jit(solution)/shard_map/ppermute | solution.py:25
  166.9 0.5 collective-permute-start.19
  167.4 0.1 collective-permute-start.21
  167.5 1.1 copy-done.21
  168.6 0.1 collective-permute-start.23
  168.7 1.0 copy-done.22
  169.8 29.8 %collective-permute-done.24.refs_6_ = bf16[384,2048]{1,0:T(8,128)(2,1)} collective-permute-done((bf16[384,2048]{1,0:T(8,128)(2,1)}, bf16[384,2048]{1,0:T(8,128)(2,1)}, u32[]{:S(2)}, u32[]{:S(2)}) %collective-permute-start.24) | collective-permute-done | bytes 1572896 | tf_op jit(solution)/shard_map/ppermute | solution.py:25
  199.5 1.1 slice.55
  200.8 1.0 copy-done.23
  201.9 1.4 copy-done.1
  203.3 1.2 copy-done.3
  204.5 1.2 copy-done.6
  205.7 8.6 %shard_map.55 = (f32[384,256]{1,0:T(8,128)S(1)}, f32[384,256]{1,0:T(8,128)}) custom-call(s32[8]{0:T(128)S(1)} %stack.35.table_ref, bf16[384,2048]{1,0:T(8,128)(2,1)S(1)} %collective-permute-done.refs_0_, bf16[384,2048]{1,0:T(8,128)(2,1)S(1)} %copy-done.1, bf16[384,2048]{1,0:T(8,128)(2,1)} %copy-done.18, bf16[384,2048]{1,0:T(8,128)(2,1)} %copy-done.21, ...), custom_call_target="tpu_custom_call" | custom-call | flops 2415919104 | bytes 15728640 | tf_op jit(solution)/shard_map/pallas_call | solution.py:118
  214.3 13.5 %collective-permute-done.16.refs_12_ = bf16[2048,256]{1,0:T(8,128)(2,1)} collective-permute-done((bf16[2048,256]{1,0:T(8,128)(2,1)}, bf16[2048,256]{1,0:T(8,128)(2,1)}, u32[]{:S(2)}, u32[]{:S(2)}) %collective-permute-start.16) | collective-permute-done | bytes 1048608 | tf_op jit(solution)/shard_map/ppermute | solution.py:25
  227.8 1.3 collective-permute-start.12
  229.1 8.6 %shard_map.56 = (f32[384,256]{1,0:T(8,128)S(1)}, f32[384,256]{1,0:T(8,128)}) custom-call(s32[8]{0:T(128)S(1)} %stack.35.table_ref, bf16[384,2048]{1,0:T(8,128)(2,1)S(1)} %collective-permute-done.refs_0_, bf16[384,2048]{1,0:T(8,128)(2,1)S(1)} %copy-done.1, bf16[384,2048]{1,0:T(8,128)(2,1)} %copy-done.18, bf16[384,2048]{1,0:T(8,128)(2,1)} %copy-done.21, ...), custom_call_target="tpu_custom_call" | custom-call | flops 2415919104 | bytes 15728640 | tf_op jit(solution)/shard_map/pallas_call | solution.py:118
  237.7 2.3 collective-permute-start.17
  240.1 7.8 %shard_map.57 = (f32[384,256]{1,0:T(8,128)S(1)}, f32[384,256]{1,0:T(8,128)S(1)}) custom-call(s32[8]{0:T(128)S(1)} %stack.35.table_ref, bf16[384,2048]{1,0:T(8,128)(2,1)S(1)} %collective-permute-done.18.refs_0_, bf16[384,2048]{1,0:T(8,128)(2,1)} %collective-permute-done.19.refs_1_, bf16[384,2048]{1,0:T(8,128)(2,1)} %collective-permute-done.20.refs_2_, ...), custom_call_target="tpu_custom_call" | custom-call | flops 2415919104 | bytes 15728640 | tf_op jit(solution)/shard_map/pallas_call | solution.py:118
  247.9 1.4 collective-permute-start.26
  249.3 8.5 %shard_map.58 = (f32[384,256]{1,0:T(8,128)S(1)}, f32[384,256]{1,0:T(8,128)}) custom-call(s32[8]{0:T(128)S(1)} %stack.35.table_ref, bf16[384,2048]{1,0:T(8,128)(2,1)S(1)} %collective-permute-done.18.refs_0_, bf16[384,2048]{1,0:T(8,128)(2,1)} %collective-permute-done.19.refs_1_, bf16[384,2048]{1,0:T(8,128)(2,1)} %collective-permute-done.20.refs_2_, ...), custom_call_target="tpu_custom_call" | custom-call | flops 2415919104 | bytes 15728640 | tf_op jit(solution)/shard_map/pallas_call | solution.py:118
  257.9 2.3 collective-permute-start.27
  260.3 1.0 add.87
  261.3 1.0 add.88
  262.4 1.0 add.89
  263.4 6.8 %collective-permute-done.27 = f32[384,256]{1,0:T(8,128)S(1)} collective-permute-done((f32[384,256]{1,0:T(8,128)}, f32[384,256]{1,0:T(8,128)S(1)}, u32[]{:S(2)}, u32[]{:S(2)}) %collective-permute-start.27) | collective-permute-done | bytes 393248 | tf_op jit(solution)/shard_map/ppermute | solution.py:25
  270.3 0.3 mul.67
  270.5 1.1 fusion
  (79 shorter events, 0.8 us)
Async XLA Ops:
  0.7 1.9 copy-start.25
  2.6 6.4 %copy-start.27 = (s32[32,4]{0,1:T(4,128)S(1)}, s32[32,4]{0,1:T(4,128)}, u32[]{:S(2)}) copy-start(s32[32,4]{0,1:T(4,128)} %param.8) | copy-start | bytes 1540
  5.0 40.9 %collective-permute-start = (bf16[384,2048]{1,0:T(8,128)(2,1)}, bf16[384,2048]{1,0:T(8,128)(2,1)S(1)}, u32[]{:S(2)}, u32[]{:S(2)}) collective-permute-start(bf16[384,2048]{1,0:T(8,128)(2,1)} %get-tuple-element.23), channel_id=1, source_target_pairs={{0,12},{1,13},{2,2},{3,3},{4,0},{5,1},{6,6},{7,7},{8,68},{9,69},{1... | collective-permute-start | bytes 4718600 | tf_op jit(solution)/shard_map/ppermute | solution.py:25
  9.3 2.3 copy-start.24
  11.6 3.2 %copy-start.26 = (bf16[384,2048]{1,0:T(8,128)(2,1)S(1)}, bf16[384,2048]{1,0:T(8,128)(2,1)}, u32[]{:S(2)}) copy-start(bf16[384,2048]{1,0:T(8,128)(2,1)} %get-tuple-element.24) | copy-start | bytes 4718596
  12.7 52.0 %copy-start.12 = (bf16[4096,256]{1,0:T(8,128)(2,1)}, bf16[4096,256]{1,0:T(8,128)(2,1)S(1)}, u32[]{:S(2)}) copy-start(bf16[4096,256]{1,0:T(8,128)(2,1)S(1)} %get-tuple-element.22.refs_8_) | copy-start | bytes 6291460
  12.7 52.0 %copy-start.13 = (bf16[4096,256]{1,0:T(8,128)(2,1)}, bf16[4096,256]{1,0:T(8,128)(2,1)S(1)}, u32[]{:S(2)}) copy-start(bf16[4096,256]{1,0:T(8,128)(2,1)S(1)} %get-tuple-element.21.refs_8_) | copy-start | bytes 6291460
  12.7 48.6 %collective-permute-start.9 = (bf16[4096,256]{1,0:T(8,128)(2,1)S(1)}, bf16[4096,256]{1,0:T(8,128)(2,1)S(1)}, u32[]{:S(2)}, u32[]{:S(2)}) collective-permute-start(bf16[4096,256]{1,0:T(8,128)(2,1)S(1)} %get-tuple-element.21.refs_8_), channel_id=1, source_target_pairs={{0,16},{1,17},{2,18},{3,19},{4,20},{5,21},{6,22},{7,23},{8,24},{9,... | collective-permute-start | bytes 6291464 | tf_op jit(solution)/shard_map/ppermute | solution.py:25
  13.4 49.7 %collective-permute-start.8 = (bf16[4096,256]{1,0:T(8,128)(2,1)S(1)}, bf16[4096,256]{1,0:T(8,128)(2,1)S(1)}, u32[]{:S(2)}, u32[]{:S(2)}) collective-permute-start(bf16[4096,256]{1,0:T(8,128)(2,1)S(1)} %get-tuple-element.21.refs_8_), channel_id=1, source_target_pairs={{0,48},{1,49},{2,50},{3,51},{4,52},{5,53},{6,54},{7,55},{8,56},{9,... | collective-permute-start | bytes 6291464 | tf_op jit(solution)/shard_map/ppermute | solution.py:25
  14.8 63.7 %collective-permute-start.18 = (bf16[384,2048]{1,0:T(8,128)(2,1)S(1)}, bf16[384,2048]{1,0:T(8,128)(2,1)S(1)}, u32[]{:S(2)}, u32[]{:S(2)}) collective-permute-start(bf16[384,2048]{1,0:T(8,128)(2,1)S(1)} %copy-done.26), channel_id=1, source_target_pairs={{0,12},{1,13},{2,2},{3,3},{4,0},{5,1},{6,6},{7,7},{8,68},{9,69},{1... | collective-permute-start | bytes 4718600 | tf_op jit(solution)/shard_map/ppermute | solution.py:25
  17.2 89.0 %collective-permute-start.14 = (bf16[4096,256]{1,0:T(8,128)(2,1)S(1)}, bf16[4096,256]{1,0:T(8,128)(2,1)S(1)}, u32[]{:S(2)}, u32[]{:S(2)}) collective-permute-start(bf16[4096,256]{1,0:T(8,128)(2,1)S(1)} %get-tuple-element.22.refs_8_), channel_id=1, source_target_pairs={{0,16},{1,17},{2,18},{3,19},{4,20},{5,21},{6,22},{7,23},{8,24},{9,... | collective-permute-start | bytes 6291464 | tf_op jit(solution)/shard_map/ppermute | solution.py:25
  45.9 62.2 %collective-permute-start.13 = (bf16[4096,256]{1,0:T(8,128)(2,1)S(1)}, bf16[4096,256]{1,0:T(8,128)(2,1)S(1)}, u32[]{:S(2)}, u32[]{:S(2)}) collective-permute-start(bf16[4096,256]{1,0:T(8,128)(2,1)S(1)} %get-tuple-element.22.refs_8_), channel_id=1, source_target_pairs={{0,48},{1,49},{2,50},{3,51},{4,52},{5,53},{6,54},{7,55},{8,56},{9,... | collective-permute-start | bytes 6291464 | tf_op jit(solution)/shard_map/ppermute | solution.py:25
  61.3 1.4 copy-start.14
  61.3 66.6 %collective-permute-start.2 = (bf16[384,2048]{1,0:T(8,128)(2,1)S(1)}, bf16[384,2048]{1,0:T(8,128)(2,1)S(1)}, u32[]{:S(2)}, u32[]{:S(2)}) collective-permute-start(bf16[384,2048]{1,0:T(8,128)(2,1)S(1)} %collective-permute-done.refs_0_), channel_id=1, source_target_pairs={{0,2},{1,3},{2,0},{3,1},{4,6},{5,7},{6,4},{7,5},{8,10},{9,11},{10,... | collective-permute-start | bytes 4718600 | tf_op jit(solution)/shard_map/ppermute | solution.py:25
  63.1 137.6 %copy-start.16 = (bf16[4096,256]{1,0:T(8,128)(2,1)}, bf16[4096,256]{1,0:T(8,128)(2,1)S(1)}, u32[]{:S(2)}) copy-start(bf16[4096,256]{1,0:T(8,128)(2,1)S(1)} %collective-permute-done.8.refs_9_) | copy-start | bytes 6291460
  63.2 64.1 %collective-permute-start.10 = (bf16[2048,256]{1,0:T(8,128)(2,1)S(1)}, bf16[2048,256]{1,0:T(8,128)(2,1)S(1)}, u32[]{:S(2)}, u32[]{:S(2)}) collective-permute-start(bf16[2048,256]{1,0:T(8,128)(2,1)S(1)} %slice.52), channel_id=1, source_target_pairs={{0,16},{1,17},{2,18},{3,19},{4,20},{5,21},{6,22},{7,23},{8,24},{9,... | collective-permute-start | bytes 3145736 | tf_op jit(solution)/shard_map/ppermute | solution.py:25
  78.4 53.9 %collective-permute-start.11 = (bf16[2048,256]{1,0:T(8,128)(2,1)S(1)}, bf16[2048,256]{1,0:T(8,128)(2,1)S(1)}, u32[]{:S(2)}, u32[]{:S(2)}) collective-permute-start(bf16[2048,256]{1,0:T(8,128)(2,1)S(1)} %slice.53), channel_id=1, source_target_pairs={{0,48},{1,49},{2,50},{3,51},{4,52},{5,53},{6,54},{7,55},{8,56},{9,... | collective-permute-start | bytes 3145736 | tf_op jit(solution)/shard_map/ppermute | solution.py:25
  106.2 94.4 %copy-start.15 = (bf16[4096,256]{1,0:T(8,128)(2,1)}, bf16[4096,256]{1,0:T(8,128)(2,1)S(1)}, u32[]{:S(2)}) copy-start(bf16[4096,256]{1,0:T(8,128)(2,1)S(1)} %collective-permute-done.14.refs_10_) | copy-start | bytes 6291460
  106.2 53.1 %collective-permute-start.4 = (bf16[384,2048]{1,0:T(8,128)(2,1)S(1)}, bf16[384,2048]{1,0:T(8,128)(2,1)S(1)}, u32[]{:S(2)}, u32[]{:S(2)}) collective-permute-start(bf16[384,2048]{1,0:T(8,128)(2,1)S(1)} %collective-permute-done.refs_0_), channel_id=1, source_target_pairs={{0,4},{1,5},{2,14},{3,15},{4,8},{5,9},{6,2},{7,3},{8,12},{9,13},{1... | collective-permute-start | bytes 4718600 | tf_op jit(solution)/shard_map/ppermute | solution.py:25
  108.1 92.6 %copy-start.17 = (bf16[4096,256]{1,0:T(8,128)(2,1)}, bf16[4096,256]{1,0:T(8,128)(2,1)S(1)}, u32[]{:S(2)}) copy-start(bf16[4096,256]{1,0:T(8,128)(2,1)S(1)} %collective-permute-done.13.refs_9_) | copy-start | bytes 6291460
  108.1 51.2 %collective-permute-start.1 = (bf16[384,2048]{1,0:T(8,128)(2,1)S(1)}, bf16[384,2048]{1,0:T(8,128)(2,1)S(1)}, u32[]{:S(2)}, u32[]{:S(2)}) collective-permute-start(bf16[384,2048]{1,0:T(8,128)(2,1)S(1)} %collective-permute-done.refs_0_), channel_id=1, source_target_pairs={{0,1},{1,0},{2,3},{3,2},{4,5},{5,4},{6,7},{7,6},{8,9},{9,8},{10,11... | collective-permute-start | bytes 4718600 | tf_op jit(solution)/shard_map/ppermute | solution.py:25
  127.3 73.4 %copy-start.2 = (bf16[2048,256]{1,0:T(8,128)(2,1)}, bf16[2048,256]{1,0:T(8,128)(2,1)S(1)}, u32[]{:S(2)}) copy-start(bf16[2048,256]{1,0:T(8,128)(2,1)S(1)} %collective-permute-done.10.refs_11_) | copy-start | bytes 3145732
  127.3 35.1 %collective-permute-start.20 = (bf16[384,2048]{1,0:T(8,128)(2,1)S(1)}, bf16[384,2048]{1,0:T(8,128)(2,1)}, u32[]{:S(2)}, u32[]{:S(2)}) collective-permute-start(bf16[384,2048]{1,0:T(8,128)(2,1)S(1)} %collective-permute-done.18.refs_0_), channel_id=1, source_target_pairs={{0,2},{1,3},{2,0},{3,1},{4,6},{5,7},{6,4},{7,5},{8,10},{9,11},{10,... | collective-permute-start | bytes 4718600 | tf_op jit(solution)/shard_map/ppermute | solution.py:25
  127.9 72.9 %copy-start.18 = (bf16[384,2048]{1,0:T(8,128)(2,1)}, bf16[384,2048]{1,0:T(8,128)(2,1)S(1)}, u32[]{:S(2)}) copy-start(bf16[384,2048]{1,0:T(8,128)(2,1)S(1)} %collective-permute-done.2.refs_2_) | copy-start | bytes 4718596
  127.9 38.9 %collective-permute-start.6 = (bf16[384,2048]{1,0:T(8,128)(2,1)S(1)}, bf16[384,2048]{1,0:T(8,128)(2,1)S(1)}, u32[]{:S(2)}, u32[]{:S(2)}) collective-permute-start(bf16[384,2048]{1,0:T(8,128)(2,1)S(1)} %collective-permute-done.2.refs_2_), channel_id=1, source_target_pairs={{16,20},{17,21},{18,30},{19,31},{20,24},{21,25},{22,18},{23,19},{2... | collective-permute-start | bytes 4718600 | tf_op jit(solution)/shard_map/ppermute | solution.py:25
  132.4 1.0 copy-start.5
  133.3 23.2 %collective-permute-start.15 = (bf16[2048,256]{1,0:T(8,128)(2,1)S(1)}, bf16[2048,256]{1,0:T(8,128)(2,1)S(1)}, u32[]{:S(2)}, u32[]{:S(2)}) collective-permute-start(bf16[2048,256]{1,0:T(8,128)(2,1)S(1)} %slice.54), channel_id=1, source_target_pairs={{0,16},{1,17},{2,18},{3,19},{4,20},{5,21},{6,22},{7,23},{8,24},{9,... | collective-permute-start | bytes 3145736 | tf_op jit(solution)/shard_map/ppermute | solution.py:25
  156.5 1.0 copy-start.8
  157.5 9.4 %collective-permute-start.22 = (bf16[384,2048]{1,0:T(8,128)(2,1)S(1)}, bf16[384,2048]{1,0:T(8,128)(2,1)}, u32[]{:S(2)}, u32[]{:S(2)}) collective-permute-start(bf16[384,2048]{1,0:T(8,128)(2,1)S(1)} %collective-permute-done.18.refs_0_), channel_id=1, source_target_pairs={{0,4},{1,5},{2,14},{3,15},{4,8},{5,9},{6,2},{7,3},{8,12},{9,13},{1... | collective-permute-start | bytes 4718600 | tf_op jit(solution)/shard_map/ppermute | solution.py:25
  159.3 41.4 %copy-start.19 = (bf16[384,2048]{1,0:T(8,128)(2,1)}, bf16[384,2048]{1,0:T(8,128)(2,1)S(1)}, u32[]{:S(2)}) copy-start(bf16[384,2048]{1,0:T(8,128)(2,1)S(1)} %collective-permute-done.4.refs_4_) | copy-start | bytes 4718596
  159.3 8.1 %collective-permute-start.3 = (bf16[384,2048]{1,0:T(8,128)(2,1)S(1)}, bf16[384,2048]{1,0:T(8,128)(2,1)S(1)}, u32[]{:S(2)}, u32[]{:S(2)}) collective-permute-start(bf16[384,2048]{1,0:T(8,128)(2,1)S(1)} %collective-permute-done.2.refs_2_), channel_id=1, source_target_pairs={{0,1},{1,0},{2,3},{3,2},{4,5},{5,4},{6,7},{7,6},{8,9},{9,8},{10,11... | collective-permute-start | bytes 4718600 | tf_op jit(solution)/shard_map/ppermute | solution.py:25
  159.3 1.2 copy-start
  160.5 7.0 %collective-permute-start.5 = (bf16[384,2048]{1,0:T(8,128)(2,1)S(1)}, bf16[384,2048]{1,0:T(8,128)(2,1)S(1)}, u32[]{:S(2)}, u32[]{:S(2)}) collective-permute-start(bf16[384,2048]{1,0:T(8,128)(2,1)S(1)} %collective-permute-done.4.refs_4_), channel_id=1, source_target_pairs={{0,1},{1,0},{2,3},{3,2},{4,5},{5,4},{6,7},{7,6},{8,9},{9,8},{10,11... | collective-permute-start | bytes 4718600 | tf_op jit(solution)/shard_map/ppermute | solution.py:25
  162.4 37.2 %collective-permute-start.24 = (bf16[384,2048]{1,0:T(8,128)(2,1)}, bf16[384,2048]{1,0:T(8,128)(2,1)}, u32[]{:S(2)}, u32[]{:S(2)}) collective-permute-start(bf16[384,2048]{1,0:T(8,128)(2,1)} %collective-permute-done.20.refs_2_), channel_id=1, source_target_pairs={{16,20},{17,21},{18,30},{19,31},{20,24},{21,25},{22,18},{23,19},{2... | collective-permute-start | bytes 4718600 | tf_op jit(solution)/shard_map/ppermute | solution.py:25
  166.8 34.0 %copy-start.20 = (bf16[384,2048]{1,0:T(8,128)(2,1)}, bf16[384,2048]{1,0:T(8,128)(2,1)S(1)}, u32[]{:S(2)}) copy-start(bf16[384,2048]{1,0:T(8,128)(2,1)S(1)} %collective-permute-done.6.refs_6_) | copy-start | bytes 4718596
  166.8 33.8 %collective-permute-start.7 = (bf16[384,2048]{1,0:T(8,128)(2,1)S(1)}, bf16[384,2048]{1,0:T(8,128)(2,1)S(1)}, u32[]{:S(2)}, u32[]{:S(2)}) collective-permute-start(bf16[384,2048]{1,0:T(8,128)(2,1)S(1)} %collective-permute-done.6.refs_6_), channel_id=1, source_target_pairs={{0,1},{1,0},{2,3},{3,2},{4,5},{5,4},{6,7},{7,6},{8,9},{9,8},{10,11... | collective-permute-start | bytes 4718600 | tf_op jit(solution)/shard_map/ppermute | solution.py:25
  166.9 70.8 %collective-permute-start.19 = (bf16[384,2048]{1,0:T(8,128)(2,1)S(1)}, bf16[384,2048]{1,0:T(8,128)(2,1)}, u32[]{:S(2)}, u32[]{:S(2)}) collective-permute-start(bf16[384,2048]{1,0:T(8,128)(2,1)S(1)} %collective-permute-done.18.refs_0_), channel_id=1, source_target_pairs={{0,1},{1,0},{2,3},{3,2},{4,5},{5,4},{6,7},{7,6},{8,9},{9,8},{10,11... | collective-permute-start | bytes 4718600 | tf_op jit(solution)/shard_map/ppermute | solution.py:25
  167.4 1.2 copy-start.21
  167.4 72.6 %collective-permute-start.21 = (bf16[384,2048]{1,0:T(8,128)(2,1)}, bf16[384,2048]{1,0:T(8,128)(2,1)}, u32[]{:S(2)}, u32[]{:S(2)}) collective-permute-start(bf16[384,2048]{1,0:T(8,128)(2,1)} %collective-permute-done.20.refs_2_), channel_id=1, source_target_pairs={{0,1},{1,0},{2,3},{3,2},{4,5},{5,4},{6,7},{7,6},{8,9},{9,8},{10,11... | collective-permute-start | bytes 4718600 | tf_op jit(solution)/shard_map/ppermute | solution.py:25
  168.6 1.1 copy-start.22
  168.6 71.4 %collective-permute-start.23 = (bf16[384,2048]{1,0:T(8,128)(2,1)}, bf16[384,2048]{1,0:T(8,128)(2,1)}, u32[]{:S(2)}, u32[]{:S(2)}) collective-permute-start(bf16[384,2048]{1,0:T(8,128)(2,1)} %collective-permute-done.22.refs_4_), channel_id=1, source_target_pairs={{0,1},{1,0},{2,3},{3,2},{4,5},{5,4},{6,7},{7,6},{8,9},{9,8},{10,11... | collective-permute-start | bytes 4718600 | tf_op jit(solution)/shard_map/ppermute | solution.py:25
  199.5 40.5 %collective-permute-start.25 = (bf16[384,2048]{1,0:T(8,128)(2,1)}, bf16[384,2048]{1,0:T(8,128)(2,1)}, u32[]{:S(2)}, u32[]{:S(2)}) collective-permute-start(bf16[384,2048]{1,0:T(8,128)(2,1)} %collective-permute-done.24.refs_6_), channel_id=1, source_target_pairs={{0,1},{1,0},{2,3},{3,2},{4,5},{5,4},{6,7},{7,6},{8,9},{9,8},{10,11... | collective-permute-start | bytes 4718600 | tf_op jit(solution)/shard_map/ppermute | solution.py:25
  200.6 1.2 copy-start.23
  200.6 27.2 %collective-permute-start.16 = (bf16[2048,256]{1,0:T(8,128)(2,1)}, bf16[2048,256]{1,0:T(8,128)(2,1)}, u32[]{:S(2)}, u32[]{:S(2)}) collective-permute-start(bf16[2048,256]{1,0:T(8,128)(2,1)} %slice.55), channel_id=1, source_target_pairs={{0,48},{1,49},{2,50},{3,51},{4,52},{5,53},{6,54},{7,55},{8,56},{9,... | collective-permute-start | bytes 3145736 | tf_op jit(solution)/shard_map/ppermute | solution.py:25
  201.9 1.4 copy-start.1
  203.3 1.2 copy-start.3
  204.5 1.2 copy-start.6
  205.7 23.4 %copy-start.9 = (bf16[2048,256]{1,0:T(8,128)(2,1)S(1)}, bf16[2048,256]{1,0:T(8,128)(2,1)}, u32[]{:S(2)}) copy-start(bf16[2048,256]{1,0:T(8,128)(2,1)} %copy-done.8) | copy-start | bytes 3145732
  227.8 12.2 %copy-start.4 = (bf16[2048,256]{1,0:T(8,128)(2,1)S(1)}, bf16[2048,256]{1,0:T(8,128)(2,1)}, u32[]{:S(2)}) copy-start(bf16[2048,256]{1,0:T(8,128)(2,1)} %copy-done.2) | copy-start | bytes 3145732
  227.8 12.2 %copy-start.7 = (bf16[2048,256]{1,0:T(8,128)(2,1)S(1)}, bf16[2048,256]{1,0:T(8,128)(2,1)}, u32[]{:S(2)}) copy-start(bf16[2048,256]{1,0:T(8,128)(2,1)} %copy-done.5) | copy-start | bytes 3145732
  227.8 32.5 %collective-permute-start.12 = (f32[384,256]{1,0:T(8,128)}, f32[384,256]{1,0:T(8,128)}, u32[]{:S(2)}, u32[]{:S(2)}) collective-permute-start(f32[384,256]{1,0:T(8,128)} %get-tuple-element.14), channel_id=1, source_target_pairs={{0,64},{1,65},{2,66},{3,67},{4,68},{5,69},{6,70},{7,71},{8,72},{9,... | collective-permute-start | bytes 1179656 | tf_op jit(solution)/shard_map/ppermute | solution.py:25
  237.7 10.2 %copy-start.10 = (f32[384,256]{1,0:T(8,128)}, f32[384,256]{1,0:T(8,128)S(1)}, u32[]{:S(2)}) copy-start(f32[384,256]{1,0:T(8,128)S(1)} %get-tuple-element.15) | copy-start | bytes 1179652
  237.7 23.6 %collective-permute-start.17 = (f32[384,256]{1,0:T(8,128)}, f32[384,256]{1,0:T(8,128)}, u32[]{:S(2)}, u32[]{:S(2)}) collective-permute-start(f32[384,256]{1,0:T(8,128)} %get-tuple-element.16), channel_id=1, source_target_pairs={{0,64},{1,65},{2,66},{3,67},{4,68},{5,69},{6,70},{7,71},{8,72},{9,... | collective-permute-start | bytes 1179656 | tf_op jit(solution)/shard_map/ppermute | solution.py:25
  247.9 12.3 %copy-start.28 = (s32[6,4]{0,1:T(4,128)S(1)}, s32[6,4]{0,1:T(4,128)}, u32[]{:S(2)}) copy-start(s32[6,4]{0,1:T(4,128)} %param.9) | copy-start | bytes 292
  247.9 13.4 %copy-start.11 = (f32[384,256]{1,0:T(8,128)S(1)}, f32[384,256]{1,0:T(8,128)}, u32[]{:S(2)}) copy-start(f32[384,256]{1,0:T(8,128)} %copy-done.10) | copy-start | bytes 1179652
  247.9 14.5 %collective-permute-start.26 = (f32[384,256]{1,0:T(8,128)S(1)}, f32[384,256]{1,0:T(8,128)}, u32[]{:S(2)}, u32[]{:S(2)}) collective-permute-start(f32[384,256]{1,0:T(8,128)S(1)} %get-tuple-element.18), channel_id=1, source_target_pairs={{0,64},{1,65},{2,66},{3,67},{4,68},{5,69},{6,70},{7,71},{8,72},{9,... | collective-permute-start | bytes 1179656 | tf_op jit(solution)/shard_map/ppermute | solution.py:25
  257.9 12.4 %collective-permute-start.27 = (f32[384,256]{1,0:T(8,128)}, f32[384,256]{1,0:T(8,128)S(1)}, u32[]{:S(2)}, u32[]{:S(2)}) collective-permute-start(f32[384,256]{1,0:T(8,128)} %get-tuple-element.20), channel_id=1, source_target_pairs={{0,64},{1,65},{2,66},{3,67},{4,68},{5,69},{6,70},{7,71},{8,72},{9,... | collective-permute-start | bytes 1179656 | tf_op jit(solution)/shard_map/ppermute | solution.py:25
